TPU v7x, 128 devices: a whole 4x4x4 slice. The times are simulated.
128 devices in a mesh: gx: 32 (over y, x, core), gy: 4 (over z).
Axes of the slice: x: 4, y: 4, z: 4, core: 2. Of those that a mesh axis runs over, the one named last changes fastest.
Arguments:
- sources: bfloat16 [8192, 8, 128], P(('gx', 'gy')), may hold values from -6 to 6
- owners: int32 [8192, 1], P(('gx', 'gy')), may hold values from 0 to 31; in each aligned block of 64 rows (0 to 63, 64 to 127, ...) at most 4 rows name the same one
- strip_rows: int32 [8192], P(('gx', 'gy')), may hold values from 0 to 255
- panel_counts: int32 [8192], P(('gx', 'gy')), may hold values from 1 to 128
- arrival_bins: int32 [8192, 4, 128], P('gx'), may hold values from 0 to 254
- arrival_fracs: float32 [8192, 4, 128], P('gx'), may hold values from 0 to 1
- gain_table: bfloat16 [8192, 8, 4, 1024], P('gx'), may hold values from -0.125 to 0.125
Outputs:
- signals: float32 [1024, 4, 256], P(('gx', 'gy'))
Inputs may be any that keep to these rules, and one draw needn't show every extreme that they name: `owners`: among the rows of one device, at most 4 strips name one patch, a bound that some block reaches.
All inputs are finite; a program needn't handle non-finite values.
Results may differ from a plain program's by a relative error of at most 0.0044.
Values may be sent and summed in bfloat16 or wider, within the bound.
A program may use at most 768 MiB of HBM per device.

v0:
```python
import jax
import jax.numpy as jnp
from jax import lax
from jax.sharding import PartitionSpec as P

NBIN = 256


def split_up(x, dim, peers):
    before, after = (x.shape[:dim], x.shape[dim + 1 :])
    return jnp.moveaxis(x.reshape(*before, peers, -1, *after), dim, 0)


def summed_on_arrival(x, axis, dim):
    parts = split_up(x, dim, lax.axis_size(axis))
    arrived = lax.all_to_all(parts, axis, split_axis=0, concat_axis=0, tiled=True)
    return arrived.sum(axis=0)


def own_tiles(x, axis, dim):
    peers = lax.axis_size(axis)
    parts = split_up(x, dim, peers)
    lines = parts.reshape(peers, -1)
    width = max(16, -(-lines.shape[1] // 1024) * 8)
    lines = jnp.pad(lines, ((0, 0), (0, width * 128 - lines.shape[1]))).reshape(-1, 128)
    own = lax.psum_scatter(lines, axis, scatter_dimension=0, tiled=True)
    return own.reshape(-1)[: parts[0].size].reshape(parts.shape[1:])


def interp_weights(bin_ids, fractions):
    positions = jnp.arange(NBIN, dtype=jnp.int32)
    lower = jnp.where(
        positions[None, None, :] == bin_ids[:, :, None], 1.0 - fractions[:, :, None], 0.0
    )
    upper = jnp.where(
        positions[None, None, :] == bin_ids[:, :, None] + 1, fractions[:, :, None], 0.0
    )
    return (lower + upper).astype(jnp.bfloat16)


def bin_rows(row_rounded, bin_ids, fractions):
    blocks = bin_ids.shape[1]
    binned = []
    for block_index in range(blocks):
        weights = interp_weights(bin_ids[:, block_index, :], fractions[:, block_index, :])
        binned.append(
            jnp.einsum("rkp,rpb->rkb", row_rounded, weights, preferred_element_type=jnp.float32)
        )
    row_count, terms = (row_rounded.shape[0], row_rounded.shape[1])
    return jnp.stack(binned, axis=2).reshape(row_count * terms, blocks, NBIN).astype(jnp.bfloat16)


def on_device(sources, owners, strip_rows, panel_counts, arrival_bins, arrival_fracs, gain_table):
    strip_count, terms, panels = sources.shape
    shards = lax.axis_size("gx")
    columns = lax.axis_size("gy")
    capacity = 2 * strip_count // shards
    live_mask = (jnp.arange(panels, dtype=jnp.int32)[None, :] < panel_counts[:, None]).astype(
        jnp.bfloat16
    )
    masked = (sources * live_mask[:, None, :]).reshape(strip_count, terms * panels)
    targets = owners[:, 0]
    target_hot = (targets[:, None] == jnp.arange(shards, dtype=jnp.int32)[None, :]).astype(
        jnp.int32
    )
    order_in = jnp.sum((jnp.cumsum(target_hot, axis=0) - 1) * target_hot, axis=1)
    slot_of = targets * capacity + order_in
    placing = jnp.arange(shards * capacity, dtype=jnp.int32)[:, None] == slot_of[None, :]
    send_sources = jnp.dot(
        placing.astype(jnp.bfloat16), masked, preferred_element_type=jnp.float32
    ).astype(jnp.bfloat16)
    send_rows = jnp.sum(placing.astype(jnp.int32) * (strip_rows + 1)[None, :], axis=1) - 1
    got_sources, got_rows = (
        lax.all_to_all(send_sources, "gx", split_axis=0, concat_axis=0, tiled=True),
        lax.all_to_all(send_rows, "gx", split_axis=0, concat_axis=0, tiled=True),
    )
    rows_here = arrival_bins.shape[0]
    row_hot = (jnp.arange(rows_here, dtype=jnp.int32)[:, None] == got_rows[None, :]).astype(
        jnp.bfloat16
    )
    row_sources = jnp.dot(row_hot, got_sources, preferred_element_type=jnp.float32)
    blocks = arrival_bins.shape[1]
    observers = gain_table.shape[3]
    share = summed_on_arrival(row_sources, "gy", 0)
    share_rows = rows_here // columns
    first = lax.axis_index("gy") * share_rows
    row_rounded = share.astype(jnp.bfloat16).reshape(share_rows, terms, panels)
    own_bins = lax.dynamic_slice_in_dim(arrival_bins, first, share_rows, 0)
    own_fracs = lax.dynamic_slice_in_dim(arrival_fracs, first, share_rows, 0)
    arrived = bin_rows(row_rounded, own_bins, own_fracs)
    own_gains = lax.dynamic_slice_in_dim(gain_table, first, share_rows, 0).reshape(
        share_rows * terms, blocks, observers
    )
    return own_tiles(
        jnp.einsum("cot,cob->tob", own_gains, arrived, preferred_element_type=jnp.float32),
        ("gx", "gy"),
        0,
    )


def solution(mesh):
    placed = (
        P(("gx", "gy"), None, None),
        P(("gx", "gy"), None),
        P(("gx", "gy")),
        P(("gx", "gy")),
        P("gx", None, None),
        P("gx", None, None),
        P("gx", None, None, None),
    )
    return jax.shard_map(
        on_device,
        mesh=mesh,
        in_specs=placed,
        out_specs=P(("gx", "gy"), None, None),
        check_vma=False,
    )
```

profile of v0, /device:TPU:1, one launch (start us, length us, event | category | flops | bytes accessed | tf_op | source)
XLA Modules:
  0.0 756.1 jit_solution(17325565656726052757)
XLA Ops:
  6.5 0.7 fusion.31
  7.4 0.8 select_reduce_fusion.1
  9.7 8.6 %all-to-all-start = ((s32[32,4,1]{1,2,0:T(1,128)}), s32[32,4,1]{1,2,0:T(1,128)S(1)}, u32[]{:S(2)}, u32[]{:S(2)}) async-start(s32[32,4,1]{1,2,0:T(1,128)} %bitcast.1), calls=%async_computation | async-start | bytes 32768 | tf_op jit(solution)/shard_map/all_to_all | solution.py:75
  18.3 0.7 fusion.32
  19.0 0.9 broadcast_multiply_fusion
  20.3 1.3 constant_dynamic-slice_fusion.4
  21.6 1.4 constant_dynamic-slice_fusion.3
  23.0 0.8 all_to_all.16
  23.8 1.4 all-to-all-done
  25.2 6.0 all-to-all-start.1
  32.5 7.5 all-to-all-done.1
  40.1 1.3 fusion.27
  41.4 4.9 all-to-all-start.2
  46.4 7.2 constant_dynamic-slice_fusion.5
  53.6 7.5 all-to-all-done.2
  61.2 7.4 fusion.17
  68.8 7.4 fusion.16
  76.3 7.4 fusion.14
  83.9 7.4 fusion.15
  91.4 7.0 fusion.7
  98.4 5.2 copy.56
  103.6 5.5 reshape.156
  109.1 638.7 %reduce-scatter.2.cloned.1.call-done = f32[64,128]{1,0:T(8,128)} async-done(((f32[8192,128]{1,0:T(8,128)}), f32[64,128]{1,0:T(8,128)}) %reduce-scatter.2.cloned.1.call-update) | async-done | bytes 32784 | tf_op jit(solution)/shard_map/reduce_scatter | solution.py:26
  747.9 1.4 reshape_reshape.4
  (27 shorter events, 4.0 us)
Async XLA Ops:
  9.7 15.5 %all-to-all-start = ((s32[32,4,1]{1,2,0:T(1,128)}), s32[32,4,1]{1,2,0:T(1,128)S(1)}, u32[]{:S(2)}, u32[]{:S(2)}) async-start(s32[32,4,1]{1,2,0:T(1,128)} %bitcast.1), calls=%async_computation | async-start | bytes 32768 | tf_op jit(solution)/shard_map/all_to_all | solution.py:75
  25.2 14.9 %all-to-all-start.1 = ((bf16[32,4,1024]{2,1,0:T(4,128)(2,1)}), bf16[32,4,1024]{2,1,0:T(4,128)(2,1)S(1)}, u32[]{:S(2)}, u32[]{:S(2)}) async-start(bf16[32,4,1024]{2,1,0:T(4,128)(2,1)} %all_to_all.16), calls=%async_computation.1 | async-start | bytes 524288 | tf_op jit(solution)/shard_map/all_to_all | solution.py:74
  41.4 19.7 %all-to-all-start.2 = ((f32[4,64,1024]{2,1,0:T(8,128)}), f32[4,64,1024]{2,1,0:T(8,128)S(1)}, u32[]{:S(2)}, u32[]{:S(2)}) async-start(f32[4,64,1024]{2,1,0:T(8,128)} %fusion.27), calls=%async_computation.2 | async-start | bytes 2097152 | tf_op jit(solution)/shard_map/all_to_all | solution.py:16
  46.4 701.5 %reduce-scatter.2.cloned.1.call-start = ((), (), s32[]{:S(2)}) async-start(), calls=%async_computation.4 | async-start | bytes 4227072 | tf_op jit(solution)/shard_map/reduce_scatter | solution.py:26
Sparse Core Ops, SparseCore 0:
  109.2 638.5 reduce-scatter.1
where the time goes:
time: 764 us; the launch traced here: 756 us
  waiting for transfers between devices  655 us (86%)
  matrix products  38.2 us (5%)
  local copies, waits for them, and re-layouts  24.7 us (3%)
  starting transfers between devices  19.5 us (3%)
  between operations  13.6 us (2%)
    reduce_scatter x1, waiting for transfers between devices, own_tiles(): own = lax.psum_scatter(lines, axis, scatter_dimension=0, tiled=True)  639 us
    dot_general x4, matrix products, bin_rows(): jnp.einsum('rkp,rpb->rkb', row_rounded, weights, preferred_element_type=j...  29.6 us
  transfers between devices with their start and end apart: 4, of which 4 were waited for; matrix products, arithmetic and copies ran while one was open for 2% of the time, Pallas kernels for 0%

commit v1 on v0

v1 whole, which is shorter than its diff:
```python
import jax
import jax.numpy as jnp
from jax import lax
from jax.experimental import pallas as pl
from jax.experimental.pallas import tpu as pltpu
from jax.sharding import PartitionSpec as P

MESH = pl.DeviceIdType.MESH
F32 = jnp.float32
BF16 = jnp.bfloat16
I32 = jnp.int32

NX = 32
NZ = 4
ND = NX * NZ
STRIPS = 64
TERMS = 8
PANELS = 128
ROWS = 256
NBIN = 256
CAP = 4
TIMES = 1024
GROUP = 16
BLOCKS = ROWS // GROUP
NT = (((1,), (1,)), ((), ()))


def iota(shape, dim):
    return lax.broadcasted_iota(I32, shape, dim)


def dot(a, b):
    return jnp.dot(a, b, preferred_element_type=F32)


def dot_nt(a, b):
    return lax.dot_general(a, b, NT, preferred_element_type=F32)


def wait_all(ref, sem):
    block = ref.at[pl.ds(0, ND - 1)]
    pltpu.make_async_copy(block, block, sem).wait()


def kernel(
    src_ref, own_ref, row_ref, cnt_ref, bins_hbm, fracs_hbm, gains_hbm, out_ref,
    send_s, send_m, got_s, got_m, bins, fracs, gains, weights, rows, spread, arrived,
    send_p, got_p, in_sem, gain_sem, ss_sem, sm_sem, sp_sem, rs_sem, rm_sem, rp_sem,
):
    mx = lax.axis_index("gx")
    mz = lax.axis_index("gy")

    def gain_copy(tile):
        return pltpu.make_async_copy(gains_hbm.at[:, tile, mz // 2], gains.at[tile], gain_sem.at[tile])

    bins_copy = pltpu.make_async_copy(bins_hbm, bins, in_sem.at[0])
    fracs_copy = pltpu.make_async_copy(fracs_hbm, fracs, in_sem.at[1])
    bins_copy.start()
    fracs_copy.start()

    owner = own_ref[...]
    row1 = row_ref[...] + 1
    hot = (iota((NX, STRIPS), 0) == owner).astype(F32)
    upto = (iota((STRIPS, STRIPS), 0) <= iota((STRIPS, STRIPS), 1)).astype(F32).astype(BF16)
    seen = dot(hot.astype(BF16), upto)
    place = jnp.sum(hot * (seen - 1.0), axis=0, keepdims=True)
    slot = owner.astype(F32) * CAP + place
    lane_of = (iota((128, STRIPS), 0) == (place.astype(I32) + mx * CAP)).astype(F32).astype(BF16)
    meta = dot_nt((hot * row1.astype(F32)).astype(BF16), lane_of)
    for j in range(NX):
        send_m[j] = meta[j : j + 1, :]
    wide = (iota((STRIPS, STRIPS * TERMS), 0) == iota((STRIPS, STRIPS * TERMS), 1) >> 3)
    wide = wide.astype(F32).astype(BF16)
    slot_c = dot(jnp.broadcast_to(slot, (8, STRIPS)).astype(BF16), wide)[0:1].astype(I32)
    tall = (iota((STRIPS * TERMS, STRIPS), 1) == iota((STRIPS * TERMS, STRIPS), 0) >> 3)
    tall = tall.astype(F32).astype(BF16)
    count = dot_nt(tall, jnp.broadcast_to(cnt_ref[...].astype(F32), (128, STRIPS)).astype(BF16))
    live = iota((STRIPS * TERMS, PANELS), 1).astype(F32) < count
    masked = jnp.where(live, src_ref[...].astype(F32), 0.0).astype(BF16)
    term = iota((1, STRIPS * TERMS), 1) & 7
    for kk in range(4):
        dest = jnp.where((term & 3) == kk, 2 * slot_c + (term >> 2), -1)
        placing = (iota((ND * 2, STRIPS * TERMS), 0) == dest).astype(F32).astype(BF16)
        placed = dot(placing, masked)
        send_s[:, :, kk * 128 : (kk + 1) * 128] = placed.reshape(NX, 8, 128).astype(BF16)

    def strip_copy(j, z):
        return pltpu.make_async_remote_copy(
            src_ref=send_s.at[j], dst_ref=got_s.at[mz * NX + mx], send_sem=ss_sem, recv_sem=rs_sem,
            device_id={"gx": j, "gy": z}, device_id_type=MESH,
        )

    def meta_copy(j, z):
        return pltpu.make_async_remote_copy(
            src_ref=send_m.at[j], dst_ref=got_m.at[mz * NX + mx], send_sem=sm_sem, recv_sem=rm_sem,
            device_id={"gx": j, "gy": z}, device_id_type=MESH,
        )

    def peer(step):
        other = lax.rem(mx * NZ + mz + step, ND)
        return other // NZ, lax.rem(other, NZ)

    @pl.loop(1, ND)
    def _(step):
        j, z = peer(step)
        strip_copy(j, z).start()
        meta_copy(j, z).start()

    got_s[mz * NX + mx] = send_s[mx]
    got_m[mz * NX + mx] = send_m[mx]

    for tile in range(8):
        gain_copy(tile).start()

    bins_copy.wait()
    fracs_copy.wait()
    where_b = iota((NBIN, PANELS), 0).astype(F32).astype(BF16)

    @pl.loop(0, ROWS // 8)
    def _(step):
        start = step * 8 * NZ + mz
        low = bins[pl.ds(start, 8, stride=NZ), :].astype(F32)
        high = low + 1.0
        frac = fracs[pl.ds(start, 8, stride=NZ), :]
        rest = 1.0 - frac
        low, high, frac, rest = (x.astype(BF16) for x in (low, high, frac, rest))
        for i in range(8):
            pick = lambda x: jnp.broadcast_to(x[i : i + 1, :], (NBIN, PANELS))
            value = jnp.where(where_b == pick(high), pick(frac), jnp.zeros((), BF16))
            value = jnp.where(where_b == pick(low), pick(rest), value)
            lanes = pl.ds(pl.multiple_of((step * 8 + i) * PANELS, PANELS), PANELS)
            weights[:, lanes] = value

    spread[...] = jnp.zeros_like(spread)

    wait_all(got_s, rs_sem)
    wait_all(got_m, rm_sem)

    half = iota((1, 2 * ND), 1) & 1
    twice = (iota((128, 2 * 128), 0) == iota((128, 2 * 128), 1) >> 1).astype(F32).astype(BF16)
    sums = [jnp.zeros((ROWS, 512), F32) for _ in range(2)]
    for z in range(NZ):
        row_of = jnp.sum(got_m[z * NX : (z + 1) * NX].reshape(NX, 128), axis=0, keepdims=True)
        row_of = dot(jnp.broadcast_to(row_of, (8, 128)).astype(BF16), twice)[0:1].astype(I32) - 1
        data = got_s[z * NX : (z + 1) * NX].reshape(NX * 8, 512)
        for h in range(2):
            hit = (iota((ROWS, 2 * 128), 0) == jnp.where(half == h, row_of, -1)).astype(F32).astype(BF16)
            sums[h] = sums[h] + dot(hit, data)
    even = lax.rem(mz, 2) == 0
    for k in range(TERMS):
        value = sums[k // 4][:, (k % 4) * 128 : (k % 4 + 1) * 128]
        rows[pl.ds(2 * k, ROWS, stride=16), :] = jnp.where(even, value, 0.0)
        rows[pl.ds(2 * k + 1, ROWS, stride=16), :] = jnp.where(even, 0.0, value)

    lane_row = iota((PANELS, 128), 1) >> 4

    @pl.loop(0, BLOCKS)
    def _(blk):
        part = rows[pl.ds(pl.multiple_of(blk * 256, 256), 256), :]
        flat = part.astype(BF16).astype(F32).T
        for g in range(GROUP):
            tile = g // 8
            piece = jnp.where(lane_row == g % 8, flat[:, tile * 128 : (tile + 1) * 128], 0.0)
            spread[g * PANELS : (g + 1) * PANELS, tile * 128 : (tile + 1) * 128] = piece.astype(BF16)
        lanes = pl.ds(pl.multiple_of(blk * GROUP * PANELS, GROUP * PANELS), GROUP * PANELS)
        value = dot(weights[:, lanes], spread[...])
        arrived[:, pl.ds(pl.multiple_of(blk * 256, 256), 256)] = value.astype(BF16)

    def part_copy(q):
        j, z = q // NZ, lax.rem(q, NZ)
        return pltpu.make_async_remote_copy(
            src_ref=send_p.at[q], dst_ref=got_p.at[mz * NX + mx], send_sem=sp_sem, recv_sem=rp_sem,
            device_id={"gx": j, "gy": z}, device_id_type=MESH,
        )

    me = mx * NZ + mz
    for turn in range(4):
        n = lax.rem(mx // 8 + turn, 4)
        for i in range(2):
            gain_copy(2 * n + i).wait()
        pair = [gains.at[2 * n + i].reshape(ROWS * TERMS * 2, 128)[...] for i in range(2)]
        value = dot(arrived[...], jnp.concatenate(pair, axis=1)).T
        send_p[pl.ds(n * 32, 32)] = value.reshape(32, 8, NBIN).astype(BF16)

        @pl.loop(0, 32)
        def _(step):
            q = n * 32 + lax.rem(me + step, 32)

            @pl.when(q != me)
            def _():
                part_copy(q).start()

    got_p[mz * NX + mx] = send_p[me]
    wait_all(got_p, rp_sem)
    for o in range(NZ):
        total = jnp.zeros((8, NBIN), F32)
        for i in range(NX):
            total = total + got_p[o * NX + i].astype(F32)
        out_ref[o] = total

    wait_all(got_s, ss_sem)
    wait_all(got_m, sm_sem)
    wait_all(got_p, sp_sem)


def on_device(sources, owners, strip_rows, panel_counts, arrival_bins, arrival_fracs, gain_table):
    any_space = pl.BlockSpec(memory_space=pl.ANY)
    vmem = pl.BlockSpec(memory_space=pltpu.VMEM)
    gains = gain_table.reshape(ROWS * TERMS, NZ, 8, 128).transpose(0, 2, 1, 3)
    gains = gains.reshape(ROWS * TERMS, 8, 2, 2, 128)
    dma = pltpu.SemaphoreType.DMA
    out = pl.pallas_call(
        kernel,
        out_shape=jax.ShapeDtypeStruct((NZ, 8, NBIN), F32),
        in_specs=[vmem, vmem, vmem, vmem, any_space, any_space, any_space],
        out_specs=vmem,
        scratch_shapes=[
            pltpu.VMEM((NX, 8, 512), BF16),
            pltpu.VMEM((NX, 1, 128), F32),
            pltpu.VMEM((ND, 8, 512), BF16),
            pltpu.VMEM((ND, 1, 128), F32),
            pltpu.VMEM((ROWS * NZ, PANELS), I32),
            pltpu.VMEM((ROWS * NZ, PANELS), F32),
            pltpu.VMEM((8, ROWS * TERMS, 2, 128), BF16),
            pltpu.VMEM((NBIN, ROWS * PANELS), BF16),
            pltpu.VMEM((ROWS * TERMS * 2, PANELS), F32),
            pltpu.VMEM((GROUP * PANELS, 256), BF16),
            pltpu.VMEM((NBIN, ROWS * TERMS * 2), BF16),
            pltpu.VMEM((ND, 8, NBIN), BF16),
            pltpu.VMEM((ND, 8, NBIN), BF16),
            dma((2,)), dma((8,)),
            dma, dma, dma, dma, dma, dma,
        ],
        compiler_params=pltpu.CompilerParams(
            has_side_effects=True, vmem_limit_bytes=60 * 1024 * 1024
        ),
    )(
        sources.reshape(STRIPS * TERMS, PANELS),
        owners.reshape(1, STRIPS),
        strip_rows.reshape(1, STRIPS),
        panel_counts.reshape(1, STRIPS),
        arrival_bins.reshape(ROWS * NZ, PANELS),
        arrival_fracs.reshape(ROWS * NZ, PANELS),
        gains,
    )
    return out.transpose(1, 0, 2)


def solution(mesh):
    placed = (
        P(("gx", "gy"), None, None),
        P(("gx", "gy"), None),
        P(("gx", "gy")),
        P(("gx", "gy")),
        P("gx", None, None),
        P("gx", None, None),
        P("gx", None, None, None),
    )
    return jax.shard_map(
        on_device,
        mesh=mesh,
        in_specs=placed,
        out_specs=P(("gx", "gy"), None, None),
        check_vma=False,
    )
```

time: 764 us -> 60.1 us (0.08); the launches traced: 756 us -> 59.9 us
  waiting for transfers between devices: 655 us -> 0 us
  Pallas kernels: 0 us -> 58.5 us
  matrix products: 38.2 us -> 0 us
  local copies, waits for them, and re-layouts: 24.7 us -> 1.39 us
  starting transfers between devices: 19.5 us -> 0 us
  between operations: 13.6 us -> 0.01 us
    reduce_scatter x1 -> x0, waiting for transfers between devices: 639 us -> none  [own_tiles(): own = lax.psum_scatter(lines, axis, scatter_dimension=0, tiled=True)]
    pallas_call x0 -> x1, Pallas kernels: none -> 58.5 us  [on_device(): pl.pallas_call(kernel, out_shape=jax.ShapeDtypeStruct((NZ, 8, NBIN), F32)...]
    dot_general x7 -> x0, matrix products: 38.2 us -> none  [the longest x4 29.6 us: bin_rows(): jnp.einsum('rkp,rpb->rkb', row_rounded, weights, preferred_element_type=j...]
    all_to_all x3 -> x0, starting transfers between devices: 19.5 us -> none  [the longest x1 8.58 us: on_device(): lax.all_to_all(send_rows, 'gx', split_axis=0, concat_axis=0, tiled=True)]
    all_to_all x3 -> x0, waiting for transfers between devices: 16.4 us -> none  [the longest x1 7.54 us: on_device(): lax.all_to_all(send_sources, 'gx', split_axis=0, concat_axis=0, tiled=True)]
  transfers between devices with their start and end apart: 4 -> 0, of which waited for: 4 -> 0; matrix products, arithmetic and copies ran while one was open for 2% -> 0% of each run, Pallas kernels for 0% -> 0%
where the time goes in v1:
time: 60.1 us; the launch traced here: 59.9 us
  Pallas kernels  58.5 us (97%)
  local copies, waits for them, and re-layouts  1.39 us (2%)
    pallas_call x1, Pallas kernels, on_device(): pl.pallas_call(kernel, out_shape=jax.ShapeDtypeStruct((NZ, 8, NBIN), F32)...  58.5 us
    transpose x1, local copies, waits for them, and re-layouts, on_device(): return out.transpose(1, 0, 2)  1.39 us

profile of v1, /device:TPU:1, one launch (start us, length us, event | category | flops | bytes accessed | tf_op | source)
XLA Modules:
  0.0 59.9 jit_solution(2873023007107568489)
XLA Ops:
  0.0 58.5 %shard_map.73 = f32[4,8,256]{2,1,0:T(8,128)} custom-call(bf16[512,128]{1,0:T(8,128)(2,1)} %bitcast.15, s32[1,64]{1,0:T(1,128)} %bitcast.17, s32[1,64]{1,0:T(1,128)} %bitcast.18, s32[1,64]{1,0:T(1,128)} %bitcast.19, s32[1024,128]{1,0:T(8,128)} %bitcast.13, f32[1024,128]{1,0:T(8,128)} %bitcast.14, bf16[2048,8,2,2,128]{4,3,2,1,0:T(2,128)(2,1)} %bitcast.12), custom_call_target="tpu_custom_call" | custom-call | tf_op jit(solution)/shard_map/pallas_call | solution.py:212
  58.5 1.4 %copy.9 = f32[8,4,256]{2,1,0:T(4,128)} copy(f32[8,4,256]{2,0,1:T(8,128)} %bitcast.16) | data formatting | bytes 65536 | tf_op jit(solution)/shard_map/transpose | solution.py:246

commit v2 on v1

v2 whole, which is shorter than its diff:
```python
import jax
import jax.numpy as jnp
from jax import lax
from jax.experimental import pallas as pl
from jax.experimental.pallas import tpu as pltpu
from jax.sharding import PartitionSpec as P

MESH = pl.DeviceIdType.MESH
F32 = jnp.float32
BF16 = jnp.bfloat16
I32 = jnp.int32

NX = 32
NZ = 4
ND = NX * NZ
STRIPS = 64
TERMS = 8
PANELS = 128
ROWS = 256
NBIN = 256
CAP = 4
TIMES = 1024
GROUP = 16
BLOCKS = ROWS // GROUP
UNROLL = 4
NT = (((1,), (1,)), ((), ()))


def iota(shape, dim):
    return lax.broadcasted_iota(I32, shape, dim)


def dot(a, b):
    return jnp.dot(a, b, preferred_element_type=F32)


def dot_nt(a, b):
    return lax.dot_general(a, b, NT, preferred_element_type=F32)


SIDES = (0, 1, 3, 2)


def wait_bytes(ref, blocks, sem):
    block = ref.at[pl.ds(0, blocks)]
    pltpu.make_async_copy(block, block, sem).wait()


def kernel(
    src_ref, own_ref, row_ref, cnt_ref, bins_hbm, fracs_hbm, gains_hbm, out_ref,
    send_s, send_m, got_s, got_m, bins, fracs, gains, weights, rows, spread, arrived,
    row_at, send_p, got_p, in_sem, gain_sem, ss_sem, sm_sem, sp_sem, rs_sem, rm_sem, rp_sem,
    zs_sem, zr_sem, za_sem, zb_sem, ms_sem, mr_sem,
):
    mx = lax.axis_index("gx")
    mz = lax.axis_index("gy")
    scopes = []

    def phase(name=None):
        if scopes:
            scopes.pop().__exit__(None, None, None)
        if name:
            scopes.append(jax.named_scope(name))
            scopes[-1].__enter__()

    def gain_copy(tile):
        return pltpu.make_async_copy(gains_hbm.at[:, tile, mz // 2], gains.at[tile], gain_sem.at[tile])

    bins_copy = pltpu.make_async_copy(bins_hbm, bins, in_sem.at[0])
    fracs_copy = pltpu.make_async_copy(fracs_hbm, fracs, in_sem.at[1])
    bins_copy.start()
    fracs_copy.start()
    for tile in range(8):
        gain_copy(tile).start()

    barrier = pltpu.get_barrier_semaphore()
    up, down, across = (lax.rem(mz + i, NZ) for i in (1, 3, 2))

    @pl.loop(1, NX)
    def _(step):
        peer = lax.rem(mx + step, NX)
        pl.semaphore_signal(barrier, inc=1, device_id={"gx": peer, "gy": mz}, device_id_type=MESH)

    for peer in (up, down, across):
        pl.semaphore_signal(barrier, inc=1, device_id={"gx": mx, "gy": peer}, device_id_type=MESH)

    def weigh(first, last):
        where_b = iota((NBIN, PANELS), 0).astype(F32).astype(BF16)

        @pl.loop(first, last)
        def _(step):
            start = step * 8 * NZ + mz
            low = bins[pl.ds(start, 8, stride=NZ), :].astype(F32)
            high = low + 1.0
            frac = fracs[pl.ds(start, 8, stride=NZ), :]
            rest = 1.0 - frac
            low, high, frac, rest = (x.astype(BF16) for x in (low, high, frac, rest))
            for i in range(8):
                pick = lambda x: jnp.broadcast_to(x[i : i + 1, :], (NBIN, PANELS))
                value = jnp.where(where_b == pick(high), pick(frac), jnp.zeros((), BF16))
                value = jnp.where(where_b == pick(low), pick(rest), value)
                lanes = pl.ds(pl.multiple_of((step * 8 + i) * PANELS, PANELS), PANELS)
                weights[:, lanes] = value

    phase("prep")
    owner = own_ref[...]
    row1 = row_ref[...] + 1
    hot = (iota((NX, STRIPS), 0) == owner).astype(F32)
    upto = (iota((STRIPS, STRIPS), 0) <= iota((STRIPS, STRIPS), 1)).astype(F32).astype(BF16)
    seen = dot(hot.astype(BF16), upto)
    place = jnp.sum(hot * (seen - 1.0), axis=0, keepdims=True)
    slot = owner.astype(F32) * CAP + place
    lane_of = (iota((128, STRIPS), 0) == (place.astype(I32) + mx * CAP)).astype(F32).astype(BF16)
    meta = dot_nt((hot * row1.astype(F32)).astype(BF16), lane_of)
    for j in range(NX):
        send_m[j] = meta[j : j + 1, :]
    wide = (iota((STRIPS, STRIPS * TERMS), 0) == iota((STRIPS, STRIPS * TERMS), 1) >> 3)
    wide = wide.astype(F32).astype(BF16)
    slot_c = dot(jnp.broadcast_to(slot, (8, STRIPS)).astype(BF16), wide)[0:1].astype(I32)
    tall = (iota((STRIPS * TERMS, STRIPS), 1) == iota((STRIPS * TERMS, STRIPS), 0) >> 3)
    tall = tall.astype(F32).astype(BF16)
    count = dot_nt(tall, jnp.broadcast_to(cnt_ref[...].astype(F32), (128, STRIPS)).astype(BF16))
    live = iota((STRIPS * TERMS, PANELS), 1).astype(F32) < count
    masked = jnp.where(live, src_ref[...].astype(F32), 0.0).astype(BF16)
    term = iota((1, STRIPS * TERMS), 1) & 7
    for kk in range(4):
        dest = jnp.where((term & 3) == kk, 2 * slot_c + (term >> 2), -1)
        placing = (iota((ND * 2, STRIPS * TERMS), 0) == dest).astype(F32).astype(BF16)
        placed = dot(placing, masked)
        send_s[:, :, kk * 128 : (kk + 1) * 128] = placed.reshape(NX, 8, 128).astype(BF16)

    phase("barrier")
    pl.semaphore_wait(barrier, NX - 1 + NZ - 1)

    my = mx // 8

    def strip_copy(j, side):
        return pltpu.make_async_remote_copy(
            src_ref=send_s.at[j], dst_ref=got_s.at[mz * NX + mx], send_sem=ss_sem,
            recv_sem=rs_sem.at[side], device_id={"gx": j, "gy": mz}, device_id_type=MESH,
        )

    def meta_copy(j):
        return pltpu.make_async_remote_copy(
            src_ref=send_m.at[j], dst_ref=got_m.at[mx], send_sem=sm_sem, recv_sem=rm_sem,
            device_id={"gx": j, "gy": mz}, device_id_type=MESH,
        )

    phase("send")
    for side in SIDES:
        for i in range(8):
            j = lax.rem(my + NZ - side, 4) * 8 + lax.rem(mx + i, 8)
            if side or i:
                strip_copy(j, side).start()

    @pl.loop(1, NX)
    def _(step):
        meta_copy(lax.rem(mx + step, NX)).start()

    got_s[mz * NX + mx] = send_s[mx]
    got_m[mx] = send_m[mx]

    def group(z, side, half=None):
        first = z * NX + lax.rem(my + side, 4) * 8
        if half is None:
            return got_s.at[pl.ds(first, 8)]
        return got_s.at[pl.ds(first + half * 4, 4)]

    def ring_copy(side, way):
        block = group(mz, side)
        return pltpu.make_async_remote_copy(
            src_ref=block, dst_ref=block, send_sem=zs_sem.at[way, side],
            recv_sem=zr_sem.at[way, side], device_id={"gx": mx, "gy": (up, down)[way]},
            device_id_type=MESH,
        )

    def relay_copy(side, way):
        block = group((down, up)[way], side, way)
        return pltpu.make_async_remote_copy(
            src_ref=block, dst_ref=block, send_sem=za_sem.at[way, side],
            recv_sem=zb_sem.at[way, side], device_id={"gx": mx, "gy": (up, down)[way]},
            device_id_type=MESH,
        )

    def weigh_some(count):
        first = done[0]
        done[0] = min(first + count, ROWS // 8)
        if done[0] > first:
            phase("weights")
            weigh(first, done[0])

    done = [0]
    bins_copy.wait()
    fracs_copy.wait()
    weigh_some(8)
    for side in SIDES:
        phase("near")
        wait_bytes(got_s, 8 if side else 7, rs_sem.at[side])
        for way in range(2):
            ring_copy(side, way).start()
        weigh_some(2)
    phase("meta")
    wait_bytes(got_m, NX - 1, rm_sem)
    row_at[mz] = jnp.sum(got_m[...].reshape(NX, 128), axis=0, keepdims=True)

    def row_copy(i):
        peer = (up, down, across)[i]
        return pltpu.make_async_remote_copy(
            src_ref=row_at.at[mz], dst_ref=row_at.at[mz], send_sem=ms_sem.at[i],
            recv_sem=mr_sem.at[i], device_id={"gx": mx, "gy": peer}, device_id_type=MESH,
        )

    for i in range(3):
        row_copy(i).start()
    for side in SIDES:
        weigh_some(4)
        phase("relay")
        for way in range(2):
            ring_copy(side, way).wait_recv()
            relay_copy(side, way).start()
    weigh_some(ROWS)
    phase("clear")
    spread[...] = jnp.zeros_like(spread)
    phase("arrive")
    for i in range(3):
        row_copy(i).wait_recv()
    for side in SIDES:
        for way in range(2):
            relay_copy(side, way).wait_recv()

    phase("sums")
    half = iota((1, 2 * ND), 1) & 1
    twice = (iota((128, 2 * 128), 0) == iota((128, 2 * 128), 1) >> 1).astype(F32).astype(BF16)
    sums = [jnp.zeros((ROWS, 512), F32) for _ in range(2)]
    for z in range(NZ):
        row_of = dot(jnp.broadcast_to(row_at[z], (8, 128)).astype(BF16), twice)[0:1].astype(I32) - 1
        data = got_s[z * NX : (z + 1) * NX].reshape(NX * 8, 512)
        for h in range(2):
            hit = (iota((ROWS, 2 * 128), 0) == jnp.where(half == h, row_of, -1)).astype(F32).astype(BF16)
            sums[h] = sums[h] + dot(hit, data)
    even = lax.rem(mz, 2) == 0
    for k in range(TERMS):
        value = sums[k // 4][:, (k % 4) * 128 : (k % 4 + 1) * 128]
        rows[pl.ds(2 * k, ROWS, stride=16), :] = jnp.where(even, value, 0.0)
        rows[pl.ds(2 * k + 1, ROWS, stride=16), :] = jnp.where(even, 0.0, value)

    phase('binning')
    lane_row = iota((PANELS, 128), 1) >> 4

    @pl.loop(0, BLOCKS // UNROLL)
    def _(turn):
        for u in range(UNROLL):
            blk = turn * UNROLL + u
            part = rows[pl.ds(pl.multiple_of(blk * 256, 256), 256), :]
            flat = part.astype(BF16).astype(F32).T
            for g in range(GROUP):
                tile = g // 8
                piece = jnp.where(lane_row == g % 8, flat[:, tile * 128 : (tile + 1) * 128], 0.0)
                spread[u, g * PANELS : (g + 1) * PANELS, tile * 128 : (tile + 1) * 128] = piece.astype(BF16)
            lanes = pl.ds(pl.multiple_of(blk * GROUP * PANELS, GROUP * PANELS), GROUP * PANELS)
            value = dot(weights[:, lanes], spread[u])
            arrived[:, pl.ds(pl.multiple_of(blk * 256, 256), 256)] = value.astype(BF16)

    def part_copy(q):
        j, z = q // NZ, lax.rem(q, NZ)
        return pltpu.make_async_remote_copy(
            src_ref=send_p.at[q], dst_ref=got_p.at[mz * NX + mx], send_sem=sp_sem, recv_sem=rp_sem,
            device_id={"gx": j, "gy": z}, device_id_type=MESH,
        )

    phase("signals")
    me = mx * NZ + mz
    for tile in range(8):
        gain_copy(tile).wait()

    def times_of(side):
        n = lax.rem(my + side, 4)
        pair = [gains.at[2 * n + i].reshape(ROWS * TERMS * 2, 128)[...] for i in range(2)]
        return dot(arrived[...], jnp.concatenate(pair, axis=1))

    def send_times(side, value):
        n = lax.rem(my + side, 4)
        send_p[pl.ds(n * 32, 32)] = value.T.reshape(32, 8, NBIN).astype(BF16)
        for step in range(0 if side else 1, 32):
            part_copy(n * 32 + lax.rem(me + step, 32)).start()

    order = (2, 1, 3, 0)
    value = times_of(order[0])
    for i in range(4):
        following = times_of(order[i + 1]) if i < 3 else None
        send_times(order[i], value)
        value = following

    phase("collect")
    got_p[mz * NX + mx] = send_p[me]
    wait_bytes(got_p, ND - 1, rp_sem)
    phase("total")
    for o in range(NZ):
        total = jnp.zeros((8, NBIN), F32)
        for i in range(NX):
            total = total + got_p[o * NX + i].astype(F32)
        out_ref[o] = total
    phase("drain")
    wait_bytes(got_s, NX - 1, ss_sem)
    wait_bytes(got_m, NX - 1, sm_sem)
    wait_bytes(got_p, ND - 1, sp_sem)
    for i in range(3):
        row_copy(i).wait_send()
    for side in SIDES:
        for way in range(2):
            ring_copy(side, way).wait_send()
            relay_copy(side, way).wait_send()
    phase()


def on_device(sources, owners, strip_rows, panel_counts, arrival_bins, arrival_fracs, gain_table):
    any_space = pl.BlockSpec(memory_space=pl.ANY)
    vmem = pl.BlockSpec(memory_space=pltpu.VMEM)
    gains = gain_table.reshape(ROWS * TERMS, NZ, 8, 128).transpose(0, 2, 1, 3)
    gains = gains.reshape(ROWS * TERMS, 8, 2, 2, 128)
    dma = pltpu.SemaphoreType.DMA
    out = pl.pallas_call(
        kernel,
        out_shape=jax.ShapeDtypeStruct((NZ, 8, NBIN), F32),
        in_specs=[vmem, vmem, vmem, vmem, any_space, any_space, any_space],
        out_specs=vmem,
        scratch_shapes=[
            pltpu.VMEM((NX, 8, 512), BF16),
            pltpu.VMEM((NX, 1, 128), F32),
            pltpu.VMEM((ND, 8, 512), BF16),
            pltpu.VMEM((NX, 1, 128), F32),
            pltpu.VMEM((ROWS * NZ, PANELS), I32),
            pltpu.VMEM((ROWS * NZ, PANELS), F32),
            pltpu.VMEM((8, ROWS * TERMS, 2, 128), BF16),
            pltpu.VMEM((NBIN, ROWS * PANELS), BF16),
            pltpu.VMEM((ROWS * TERMS * 2, PANELS), F32),
            pltpu.VMEM((UNROLL, GROUP * PANELS, 256), BF16),
            pltpu.VMEM((NBIN, ROWS * TERMS * 2), BF16),
            pltpu.VMEM((NZ, 1, 128), F32),
            pltpu.VMEM((ND, 8, NBIN), BF16),
            pltpu.VMEM((ND, 8, NBIN), BF16),
            dma((2,)), dma((8,)), dma, dma, dma, dma((4,)), dma, dma,
            dma((2, 4)), dma((2, 4)), dma((2, 4)), dma((2, 4)), dma((3,)), dma((3,)),
        ],
        compiler_params=pltpu.CompilerParams(
            collective_id=0, has_side_effects=True, vmem_limit_bytes=60 * 1024 * 1024
        ),
    )(
        sources.reshape(STRIPS * TERMS, PANELS),
        owners.reshape(1, STRIPS),
        strip_rows.reshape(1, STRIPS),
        panel_counts.reshape(1, STRIPS),
        arrival_bins.reshape(ROWS * NZ, PANELS),
        arrival_fracs.reshape(ROWS * NZ, PANELS),
        gains,
    )
    return out.transpose(1, 0, 2)


def solution(mesh):
    placed = (
        P(("gx", "gy"), None, None),
        P(("gx", "gy"), None),
        P(("gx", "gy")),
        P(("gx", "gy")),
        P("gx", None, None),
        P("gx", None, None),
        P("gx", None, None, None),
    )
    return jax.shard_map(
        on_device,
        mesh=mesh,
        in_specs=placed,
        out_specs=P(("gx", "gy"), None, None),
        check_vma=False,
    )
```

time: 60.1 us -> 47.9 us (0.80)
  Pallas kernels: 58.5 us -> 46.3 us
    pallas_call x1, Pallas kernels: 58.5 us -> 46.3 us  [on_device(): pl.pallas_call(kernel, out_shape=jax.ShapeDtypeStruct((NZ, 8, NBIN), F32)...]
where the time goes in v2:
time: 47.9 us; the launch traced here: 47.7 us
  Pallas kernels  46.3 us (97%)
  local copies, waits for them, and re-layouts  1.39 us (3%)
    pallas_call x1, Pallas kernels, on_device(): pl.pallas_call(kernel, out_shape=jax.ShapeDtypeStruct((NZ, 8, NBIN), F32)...  46.3 us
    transpose x1, local copies, waits for them, and re-layouts, on_device(): return out.transpose(1, 0, 2)  1.39 us

profile of v2, /device:TPU:1, one launch (start us, length us, event | category | flops | bytes accessed | tf_op | source)
XLA Modules:
  0.0 47.7 jit_solution(1466552675629651468)
XLA Ops:
  0.0 46.3 %shard_map.73 = f32[4,8,256]{2,1,0:T(8,128)} custom-call(bf16[512,128]{1,0:T(8,128)(2,1)} %bitcast.15, s32[1,64]{1,0:T(1,128)} %bitcast.17, s32[1,64]{1,0:T(1,128)} %bitcast.18, s32[1,64]{1,0:T(1,128)} %bitcast.19, s32[1024,128]{1,0:T(8,128)} %bitcast.13, f32[1024,128]{1,0:T(8,128)} %bitcast.14, bf16[2048,8,2,2,128]{4,3,2,1,0:T(2,128)(2,1)} %bitcast.12), custom_call_target="tpu_custom_call" | custom-call | tf_op jit(solution)/shard_map/pallas_call | solution.py:322
  46.3 1.4 %copy.9 = f32[8,4,256]{2,1,0:T(4,128)} copy(f32[8,4,256]{2,0,1:T(8,128)} %bitcast.16) | data formatting | bytes 65536 | tf_op jit(solution)/shard_map/transpose | solution.py:357
